TPU v7x, 32 devices: a whole 2x2x4 slice. The times are simulated.
32 devices in a mesh: rows: 8 (over z, y), cols: 4 (over x, core).
Axes of the slice: x: 2, y: 2, z: 4, core: 2. Of those that a mesh axis runs over, the one named last changes fastest.
Arguments:
- points: bfloat16 [4096, 256], P(('rows', 'cols')), may hold values from -6 to 6
- start_vectors: float32 [8, 4096], P(None, ('rows', 'cols')), may hold values from -6 to 6
- degree: bfloat16 [4096], P(('rows', 'cols')), may hold values from 0.19921875 to 2
Outputs:
- embedding: float32 [8, 4096], P(None, ('rows', 'cols'))
All inputs are finite; a program needn't handle non-finite values.
Results may differ from a plain program's by a relative error of at most 0.0034.
Values may be sent and summed in bfloat16 or wider, within the bound.
A program may use at most 64 MiB of HBM per device.

v0:
```python
import jax
import jax.numpy as jnp
from jax import lax
from jax.sharding import PartitionSpec as P

ITERS = 3


def body(points, start_vectors, degree):
    row_count = lax.axis_size("rows")
    col_count = lax.axis_size("cols")
    row_place = lax.axis_index("rows")
    col_place = lax.axis_index("cols")
    span_size = points.shape[0]
    sharpness = 4.0 / points.shape[1]
    row_points, row_degree = (
        lax.all_gather(points, "cols", axis=0, tiled=True),
        lax.all_gather(degree, "cols", axis=0, tiled=True),
    )
    row_total = row_points.shape[0]
    row_float = row_points.astype(jnp.float32)
    row_norms = jnp.sum(row_float * row_float, axis=1)
    row_slots = jnp.arange(row_total, dtype=jnp.int32)
    row_global = (
        row_place * col_count + row_slots // span_size
    ) * span_size + row_slots % span_size

    def kernel_block(x_block, col_norms, first_slot):
        inner = lax.dot_general(
            row_points, x_block, (((1,), (1,)), ((), ())), preferred_element_type=jnp.float32
        )
        distance = row_norms[:, None] + col_norms[None, :] - 2.0 * inner
        kernel = jnp.exp(-sharpness * distance)
        col_slots = first_slot + jnp.arange(x_block.shape[0], dtype=jnp.int32)
        col_global = (
            col_slots // span_size * col_count + col_place
        ) * span_size + col_slots % span_size
        return jnp.where(
            row_global[:, None] == col_global[None, :], jnp.float32(0.0), kernel
        ).astype(jnp.bfloat16)

    vectors = start_vectors
    for iteration in range(ITERS):
        empty = jnp.zeros((vectors.shape[0], row_total), jnp.float32)
        sending = vectors.T.astype(jnp.bfloat16)
        x_piece = lax.all_gather(points, "rows", axis=0, tiled=True)
        v_piece = lax.all_gather(sending, "rows", axis=0, tiled=True)
        piece_rows = x_piece.shape[0]
        block_size = 512
        block_count = piece_rows // block_size

        def accumulate(block_index, running):
            offset = block_index * block_size
            x_block = lax.dynamic_slice_in_dim(x_piece, offset, block_size, 0)
            v_block = lax.dynamic_slice_in_dim(v_piece, offset, block_size, 0)
            x_float = x_block.astype(jnp.float32)
            col_norms = jnp.sum(x_float * x_float, axis=1)
            kernel = kernel_block(x_block, col_norms, offset)
            return running + lax.dot_general(
                v_block, kernel, (((0,), (1,)), ((), ())), preferred_element_type=jnp.float32
            )

        partial_value = lax.fori_loop(0, block_count, accumulate, empty)
        summed = lax.psum(partial_value, "cols")
        row_state = summed / row_degree.astype(jnp.float32)[None, :]
        vectors = lax.dynamic_slice_in_dim(row_state, col_place * span_size, span_size, 1)
    magnitude = lax.psum(jnp.sum(jnp.abs(row_state), axis=1), "rows")
    mean_abs = magnitude / (span_size * row_count * col_count)
    return vectors / (mean_abs[:, None] + 1e-06)


def solution(mesh):
    return jax.shard_map(
        body,
        mesh=mesh,
        in_specs=(P(("rows", "cols"), None), P(None, ("rows", "cols")), P(("rows", "cols"))),
        out_specs=P(None, ("rows", "cols")),
        check_vma=False,
    )
```

profile of v0, /device:TPU:0, one launch (start us, length us, event | category | flops | bytes accessed | tf_op | source)
XLA Modules:
  0.0 177.6 jit_solution(2372064318550203494)
XLA Ops:
  0.0 0.0 copy-start.2
  0.0 0.7 copy-done.2
  0.7 6.0 %all-gather = bf16[4,1,128]{2,1,0:T(2,128)(2,1)S(1)} all-gather(bf16[1,1,128]{2,1,0:T(2,128)(2,1)S(1)} %bitcast.73), channel_id=1, replica_groups=mesh['rows'=8,'cols'=4] {'cols'}, dimensions={0}, use_global_device_ids=true | all-gather | bytes 1280 | tf_op jit(solution)/shard_map/all_gather | solution.py:18
  6.7 0.1 dynamic-slice
  6.7 6.5 %all_gather.21 = bf16[512,256]{1,0:T(8,128)(2,1)S(1)} all-gather(bf16[128,256]{1,0:T(8,128)(2,1)} %param.9), channel_id=1, replica_groups=mesh['rows'=8,'cols'=4] {'cols'}, dimensions={0}, use_global_device_ids=true | all-gather | bytes 327680 | tf_op jit(solution)/shard_map/all_gather | solution.py:17
  13.2 0.0 copy-start
  13.2 0.1 multiply_reduce_fusion.3
  13.4 0.7 copy-done
  14.0 0.0 copy-start.1
  14.0 32.1 %all_gather.22 = bf16[1024,256]{1,0:T(8,128)(2,1)S(1)} all-gather(bf16[128,256]{1,0:T(8,128)(2,1)S(1)} %copy-done), channel_id=1, replica_groups=mesh['rows'=8,'cols'=4] {'rows'}, dimensions={0}, use_global_device_ids=true | all-gather | bytes 589824 | tf_op jit(solution)/shard_map/all_gather | solution.py:46
  46.2 0.0 copy-done.1
  46.2 26.1 %all_gather.20 = bf16[1024,8]{0,1:T(8,128)(2,1)S(1)} all-gather(bf16[128,8]{0,1:T(8,128)(2,1)S(1)} %convert_bitcast_fusion), channel_id=1, replica_groups=mesh['rows'=8,'cols'=4] {'rows'}, dimensions={0}, use_global_device_ids=true | all-gather | bytes 18432 | tf_op jit(solution)/shard_map/all_gather | solution.py:47
  72.3 1.6 while.48
  72.3 0.1 multiply_reduce_fusion.7
  72.5 0.6 fusion.155
  73.1 0.2 multiply_reduce_fusion.7
  73.3 0.6 fusion.155
  73.9 10.1 %psum.28 = f32[8,512]{1,0:T(8,128)S(1)} all-reduce(f32[8,512]{1,0:T(8,128)S(1)} %get-tuple-element.608), channel_id=1, replica_groups=mesh['rows'=8,'cols'=4] {'cols'}, use_global_device_ids=true, to_apply=%region_4.5 | all-reduce | flops 4096 | bytes 32768 | tf_op jit(solution)/shard_map/psum | solution.py:64
  84.0 26.1 %all_gather.24 = bf16[1024,8]{0,1:T(8,128)(2,1)S(1)} all-gather(bf16[128,8]{0,1:T(8,128)(2,1)S(1)} %fusion.131), channel_id=1, replica_groups=mesh['rows'=8,'cols'=4] {'rows'}, dimensions={0}, use_global_device_ids=true | all-gather | bytes 18432 | tf_op jit(solution)/shard_map/all_gather | solution.py:47
  110.1 1.6 while.49
  110.1 0.1 multiply_reduce_fusion.8
  110.3 0.6 fusion.160
  110.9 0.2 multiply_reduce_fusion.8
  111.1 0.6 fusion.160
  111.7 10.1 %psum.29 = f32[8,512]{1,0:T(8,128)S(1)} all-reduce(f32[8,512]{1,0:T(8,128)S(1)} %get-tuple-element.609), channel_id=1, replica_groups=mesh['rows'=8,'cols'=4] {'cols'}, use_global_device_ids=true, to_apply=%region_8.9 | all-reduce | flops 4096 | bytes 32768 | tf_op jit(solution)/shard_map/psum | solution.py:64
  121.8 26.1 %all_gather.25 = bf16[1024,8]{0,1:T(8,128)(2,1)S(1)} all-gather(bf16[128,8]{0,1:T(8,128)(2,1)S(1)} %fusion.132), channel_id=1, replica_groups=mesh['rows'=8,'cols'=4] {'rows'}, dimensions={0}, use_global_device_ids=true | all-gather | bytes 18432 | tf_op jit(solution)/shard_map/all_gather | solution.py:47
  148.0 1.6 while.50
  148.0 0.1 multiply_reduce_fusion.9
  148.1 0.6 fusion.165
  148.7 0.2 multiply_reduce_fusion.9
  148.9 0.6 fusion.165
  149.5 10.1 %psum.30 = f32[8,512]{1,0:T(8,128)S(1)} all-reduce(f32[8,512]{1,0:T(8,128)S(1)} %get-tuple-element.610), channel_id=1, replica_groups=mesh['rows'=8,'cols'=4] {'cols'}, use_global_device_ids=true, to_apply=%region_12.13 | all-reduce | flops 4096 | bytes 32768 | tf_op jit(solution)/shard_map/psum | solution.py:64
  159.7 0.1 abs_reduce_fusion
  159.8 17.1 %psum.31 = f32[8]{0:T(128)S(1)} all-reduce(f32[8]{0:T(128)S(1)} %get-tuple-element.749), channel_id=1, replica_groups=mesh['rows'=8,'cols'=4] {'rows'}, use_global_device_ids=true, to_apply=%region_14.15 | all-reduce | flops 8 | bytes 64 | tf_op jit(solution)/shard_map/psum | solution.py:67
  176.9 0.7 dynamic-slice_divide_fusion.2
  (14 shorter events, 0.1 us)
Async XLA Ops:
  0.0 0.7 copy-start.2
  13.2 0.8 copy-start
  14.0 32.1 %copy-start.1 = (f32[8,128]{1,0:T(8,128)S(1)}, f32[8,128]{1,0:T(8,128)}, u32[]{:S(2)}) copy-start(f32[8,128]{1,0:T(8,128)} %param.10) | copy-start | bytes 12292
where the time goes:
time: 178 us
  blocking collectives  170 us (96%)
  matrix products  3.57 us (2%)
  other arithmetic  2.03 us (1%)
    all_gather x3, blocking collectives, body(): v_piece = lax.all_gather(sending, 'rows', axis=0, tiled=True)  78.3 us
    all_gather x1, blocking collectives, body(): x_piece = lax.all_gather(points, 'rows', axis=0, tiled=True)  32.1 us
    psum x3, blocking collectives, body(): summed = lax.psum(partial_value, 'cols')  30.4 us
    psum x1, blocking collectives, body(): magnitude = lax.psum(jnp.sum(jnp.abs(row_state), axis=1), 'rows')  17.1 us
    all_gather x1, blocking collectives, body(): lax.all_gather(points, 'cols', axis=0, tiled=True)  6.47 us
    all_gather x1, blocking collectives, body(): lax.all_gather(degree, 'cols', axis=0, tiled=True)  5.99 us
    dot_general x6, matrix products, accumulate(): lax.dot_general(v_block, kernel, (((0,), (1,)), ((), ())), preferred_elem...  3.57 us

commit v1 on v0

--- a/solution.py
+++ b/solution.py
@@ -61,7 +61,14 @@
             )
 
         partial_value = lax.fori_loop(0, block_count, accumulate, empty)
-        summed = lax.psum(partial_value, "cols")
+        devs = lax.axis_size("cols")
+        summed = partial_value
+        for jj in [j0 for j0 in (1, 2, 4, 8, 16) if j0 < devs]:
+            ledger = []
+            for ii in range(devs):
+                ledger.append((ii, ii ^ jj))
+            all_rows = lax.ppermute(summed, axis_name="cols", perm=ledger)
+            summed = summed + all_rows
         row_state = summed / row_degree.astype(jnp.float32)[None, :]
         vectors = lax.dynamic_slice_in_dim(row_state, col_place * span_size, span_size, 1)
     magnitude = lax.psum(jnp.sum(jnp.abs(row_state), axis=1), "rows")

time: 178 us -> 160 us (0.90)
  blocking collectives: 170 us -> 140 us
  waiting for transfers between devices: 0 us -> 10 us
  starting transfers between devices: 0 us -> 2.56 us
    psum x3 -> x0, blocking collectives: 30.4 us -> none  [body(): summed = lax.psum(partial_value, 'cols')]
    ppermute x0 -> x6, waiting for transfers between devices: none -> 10 us  [body(): all_rows = lax.ppermute(summed, axis_name='cols', perm=ledger)]
    ppermute x0 -> x6, starting transfers between devices: none -> 2.56 us  [body(): all_rows = lax.ppermute(summed, axis_name='cols', perm=ledger)]
  transfers between devices with their start and end apart: 0 -> 6, of which waited for: 0 -> 5; matrix products, arithmetic and copies ran while one was open for 0% -> 0% of each run, Pallas kernels for 0% -> 0%
where the time goes in v1:
time: 160 us
  blocking collectives  140 us (88%)
  waiting for transfers between devices  10 us (6%)
  matrix products  3.57 us (2%)
  starting transfers between devices  2.56 us (2%)
  other arithmetic  2.04 us (1%)
    all_gather x3, blocking collectives, body(): v_piece = lax.all_gather(sending, 'rows', axis=0, tiled=True)  78.3 us
    all_gather x1, blocking collectives, body(): x_piece = lax.all_gather(points, 'rows', axis=0, tiled=True)  31.9 us
    psum x1, blocking collectives, body(): magnitude = lax.psum(jnp.sum(jnp.abs(row_state), axis=1), 'rows')  17.1 us
    ppermute x6, waiting for transfers between devices, body(): all_rows = lax.ppermute(summed, axis_name='cols', perm=ledger)  10 us
    all_gather x1, blocking collectives, body(): lax.all_gather(points, 'cols', axis=0, tiled=True)  7.55 us
    all_gather x1, blocking collectives, body(): lax.all_gather(degree, 'cols', axis=0, tiled=True)  5.05 us
    dot_general x6, matrix products, accumulate(): lax.dot_general(v_block, kernel, (((0,), (1,)), ((), ())), preferred_elem...  3.57 us
  transfers between devices with their start and end apart: 6, of which 5 were waited for; matrix products, arithmetic and copies ran while one was open for 0% of the time, Pallas kernels for 0%

profile of v1, /device:TPU:0, one launch (start us, length us, event | category | flops | bytes accessed | tf_op | source)
XLA Modules:
  0.0 159.7 jit_solution(17150227175480588680)
XLA Ops:
  0.0 0.0 copy-start
  0.0 7.5 %all_gather.21 = bf16[512,256]{1,0:T(8,128)(2,1)S(1)} all-gather(bf16[128,256]{1,0:T(8,128)(2,1)} %param.9), channel_id=1, replica_groups=mesh['rows'=8,'cols'=4] {'cols'}, dimensions={0}, use_global_device_ids=true | all-gather | bytes 327680 | tf_op jit(solution)/shard_map/all_gather | solution.py:17
  7.6 0.0 copy-done
  7.6 31.9 %all_gather.22 = bf16[1024,256]{1,0:T(8,128)(2,1)S(1)} all-gather(bf16[128,256]{1,0:T(8,128)(2,1)S(1)} %copy-done), channel_id=1, replica_groups=mesh['rows'=8,'cols'=4] {'rows'}, dimensions={0}, use_global_device_ids=true | all-gather | bytes 589824 | tf_op jit(solution)/shard_map/all_gather | solution.py:46
  39.5 0.1 multiply_reduce_fusion.3
  39.6 0.0 copy-start.1
  39.7 0.7 copy-done.1
  40.3 26.1 %all_gather.20 = bf16[1024,8]{0,1:T(8,128)(2,1)S(1)} all-gather(bf16[128,8]{0,1:T(8,128)(2,1)S(1)} %convert_bitcast_fusion), channel_id=1, replica_groups=mesh['rows'=8,'cols'=4] {'rows'}, dimensions={0}, use_global_device_ids=true | all-gather | bytes 18432 | tf_op jit(solution)/shard_map/all_gather | solution.py:47
  66.4 1.6 while.48
  66.4 0.1 multiply_reduce_fusion.7
  66.6 0.6 fusion.157
  67.2 0.2 multiply_reduce_fusion.7
  67.4 0.6 fusion.157
  68.0 0.0 collective-permute-start
  68.0 1.2 collective-permute-done
  69.2 1.5 collective-permute-start.1
  70.7 0.0 copy-start.2
  70.7 0.7 copy-done.2
  71.4 5.0 %all-gather = bf16[4,1,128]{2,1,0:T(2,128)(2,1)S(1)} all-gather(bf16[1,1,128]{2,1,0:T(2,128)(2,1)S(1)} %bitcast.73), channel_id=1, replica_groups=mesh['rows'=8,'cols'=4] {'cols'}, dimensions={0}, use_global_device_ids=true | all-gather | bytes 1280 | tf_op jit(solution)/shard_map/all_gather | solution.py:18
  76.4 0.1 dynamic-slice
  76.5 0.0 collective-permute-done.1
  76.5 26.1 %all_gather.24 = bf16[1024,8]{0,1:T(8,128)(2,1)S(1)} all-gather(bf16[128,8]{0,1:T(8,128)(2,1)S(1)} %fusion.133), channel_id=1, replica_groups=mesh['rows'=8,'cols'=4] {'rows'}, dimensions={0}, use_global_device_ids=true | all-gather | bytes 18432 | tf_op jit(solution)/shard_map/all_gather | solution.py:47
  102.6 1.6 while.49
  102.6 0.1 multiply_reduce_fusion.8
  102.8 0.6 fusion.162
  103.4 0.2 multiply_reduce_fusion.8
  103.6 0.6 fusion.162
  104.2 0.0 collective-permute-start.2
  104.2 1.2 collective-permute-done.2
  105.4 0.5 collective-permute-start.3
  106.0 3.2 %collective-permute-done.3 = f32[8,512]{1,0:T(8,128)S(1)} collective-permute-done((f32[8,512]{1,0:T(8,128)S(1)}, f32[8,512]{1,0:T(8,128)S(1)}, u32[]{:S(2)}, u32[]{:S(2)}) %collective-permute-start.3) | collective-permute-done | bytes 16416 | tf_op jit(solution)/shard_map/ppermute | solution.py:70
  109.2 26.1 %all_gather.25 = bf16[1024,8]{0,1:T(8,128)(2,1)S(1)} all-gather(bf16[128,8]{0,1:T(8,128)(2,1)S(1)} %fusion.134), channel_id=1, replica_groups=mesh['rows'=8,'cols'=4] {'rows'}, dimensions={0}, use_global_device_ids=true | all-gather | bytes 18432 | tf_op jit(solution)/shard_map/all_gather | solution.py:47
  135.3 1.6 while.50
  135.3 0.1 multiply_reduce_fusion.9
  135.5 0.6 fusion.167
  136.1 0.2 multiply_reduce_fusion.9
  136.3 0.6 fusion.167
  136.8 0.0 collective-permute-start.4
  136.8 1.2 collective-permute-done.4
  138.1 0.5 collective-permute-start.5
  138.6 3.2 %collective-permute-done.5 = f32[8,512]{1,0:T(8,128)S(1)} collective-permute-done((f32[8,512]{1,0:T(8,128)S(1)}, f32[8,512]{1,0:T(8,128)S(1)}, u32[]{:S(2)}, u32[]{:S(2)}) %collective-permute-start.5) | collective-permute-done | bytes 16416 | tf_op jit(solution)/shard_map/ppermute | solution.py:70
  141.8 0.1 abs_reduce_fusion
  141.9 17.1 %psum.7 = f32[8]{0:T(128)S(1)} all-reduce(f32[8]{0:T(128)S(1)} %get-tuple-element.749), channel_id=1, replica_groups=mesh['rows'=8,'cols'=4] {'rows'}, use_global_device_ids=true, to_apply=%region_11.12 | all-reduce | flops 8 | bytes 64 | tf_op jit(solution)/shard_map/psum | solution.py:74
  159.1 0.7 dynamic-slice_divide_fusion
  (17 shorter events, 0.1 us)
Async XLA Ops:
  0.0 7.6 %copy-start = (bf16[128,256]{1,0:T(8,128)(2,1)S(1)}, bf16[128,256]{1,0:T(8,128)(2,1)}, u32[]{:S(2)}) copy-start(bf16[128,256]{1,0:T(8,128)(2,1)} %param.9) | copy-start | bytes 196612
  39.6 0.7 copy-start.1
  68.0 1.2 collective-permute-start
  69.2 7.3 %collective-permute-start.1 = (f32[8,512]{1,0:T(8,128)S(1)}, f32[8,512]{1,0:T(8,128)S(1)}, u32[]{:S(2)}, u32[]{:S(2)}) collective-permute-start(f32[8,512]{1,0:T(8,128)S(1)} %add.529), channel_id=1, source_target_pairs={{0,2},{1,3},{2,0},{3,1},{4,6},{5,7},{6,4},{7,5},{8,10},{9,11},{10,... | collective-permute-start | bytes 49160 | tf_op jit(solution)/shard_map/ppermute | solution.py:70
  70.7 0.7 copy-start.2
  104.2 1.2 collective-permute-start.2
  105.4 3.7 %collective-permute-start.3 = (f32[8,512]{1,0:T(8,128)S(1)}, f32[8,512]{1,0:T(8,128)S(1)}, u32[]{:S(2)}, u32[]{:S(2)}) collective-permute-start(f32[8,512]{1,0:T(8,128)S(1)} %add.532), channel_id=1, source_target_pairs={{0,2},{1,3},{2,0},{3,1},{4,6},{5,7},{6,4},{7,5},{8,10},{9,11},{10,... | collective-permute-start | bytes 49160 | tf_op jit(solution)/shard_map/ppermute | solution.py:70
  136.8 1.2 collective-permute-start.4
  138.1 3.7 %collective-permute-start.5 = (f32[8,512]{1,0:T(8,128)S(1)}, f32[8,512]{1,0:T(8,128)S(1)}, u32[]{:S(2)}, u32[]{:S(2)}) collective-permute-start(f32[8,512]{1,0:T(8,128)S(1)} %add.534), channel_id=1, source_target_pairs={{0,2},{1,3},{2,0},{3,1},{4,6},{5,7},{6,4},{7,5},{8,10},{9,11},{10,... | collective-permute-start | bytes 49160 | tf_op jit(solution)/shard_map/ppermute | solution.py:70
